TPU v7x, 32 devices: a whole 2x2x4 slice. The times are simulated.
32 devices in a mesh: expert: 4 (over y, core), shard: 8 (over z, x).
Axes of the slice: x: 2, y: 2, z: 4, core: 2. Of those that a mesh axis runs over, the one named last changes fastest.
Arguments:
- w_gate: float32 [128, 2048, 768], P('expert', 'shard'), may hold values from -0.1875 to 0.1875
- w_up: float32 [128, 2048, 768], P('expert', 'shard'), may hold values from -0.1875 to 0.1875
- router_weight: float32 [2048, 128], P('shard', 'expert'), may hold values from -0.125 to 0.125
- router_gain: float32 [2048], P('shard'), may hold values from 0.25 to 1.75
Outputs:
- serve_gate: bfloat16 [128, 2048, 768], P('expert', None, 'shard')
- serve_up: bfloat16 [128, 2048, 768], P('expert', None, 'shard')
- scale_gate: float32 [128, 768], P('expert', 'shard')
- scale_up: float32 [128, 768], P('expert', 'shard')
- serve_router: bfloat16 [2048, 128], replicated
All inputs are finite; a program needn't handle non-finite values. Where the computation divides by a largest or mean magnitude, that divisor is 1e-20 or more.
Results may differ from a plain program's by a relative error of at most 0.001.
Values may be sent and summed in bfloat16 or wider, within the bound.
A program may use at most 192 MiB of HBM per device.

v0:
```python
import jax
import jax.numpy as jnp
from jax import lax
from jax.sharding import PartitionSpec as P


def body(w_gate, w_up, router_weight, router_gain):
    scale_gate, scale_up = lax.pmax(
        (jnp.max(jnp.abs(w_gate), axis=1), jnp.max(jnp.abs(w_up), axis=1)), "shard"
    )
    narrow_gate, narrow_up = (
        (w_gate / jnp.expand_dims(scale_gate, 1)).astype(jnp.bfloat16),
        (w_up / jnp.expand_dims(scale_up, 1)).astype(jnp.bfloat16),
    )
    serve_gate, serve_up = (
        lax.all_to_all(narrow_gate, "shard", split_axis=2, concat_axis=1, tiled=True),
        lax.all_to_all(narrow_up, "shard", split_axis=2, concat_axis=1, tiled=True),
    )
    scale_gate = lax.dynamic_slice_in_dim(
        scale_gate, lax.axis_index("shard") * serve_gate.shape[2], serve_gate.shape[2], axis=1
    )
    scale_up = lax.dynamic_slice_in_dim(
        scale_up, lax.axis_index("shard") * serve_up.shape[2], serve_up.shape[2], axis=1
    )
    part_router = (router_weight * router_gain[:, None]).astype(jnp.bfloat16)
    row_router = lax.all_gather(part_router, "shard", axis=0, tiled=True)
    serve_router = lax.all_gather(row_router, "expert", axis=1, tiled=True)
    return (serve_gate, serve_up, scale_gate, scale_up, serve_router)


def solution(mesh):
    return jax.shard_map(
        body,
        mesh=mesh,
        in_specs=(
            P("expert", "shard", None),
            P("expert", "shard", None),
            P("shard", "expert"),
            P("shard"),
        ),
        out_specs=(
            P("expert", None, "shard"),
            P("expert", None, "shard"),
            P("expert", "shard"),
            P("expert", "shard"),
            P(),
        ),
        check_vma=False,
    )
```

profile of v0, /device:TPU:0, one launch (start us, length us, event | category | flops | bytes accessed | tf_op | source)
XLA Modules:
  0.0 771.9 jit_solution(16742101143083610115)
XLA Ops:
  7.2 0.0 all-reduce.3.cloned.1.call-start
  7.2 0.0 copy-start
  7.2 10.2 %abs_reduce_fusion = f32[32,768]{1,0:T(8,128)} fusion(f32[32,256,768]{2,1,0:T(8,128)} %param.5), kind=kLoop, calls=%fused_computation.1 | loop fusion | flops 12558336 | bytes 25264128 | tf_op jit(solution)/shard_map/reduce_max | solution.py:9
  17.4 5.3 copy-done
  22.7 3.0 abs_reduce_fusion.1
  25.7 0.0 all-reduce.3.cloned.1.call-update
  25.7 25.1 %copy.21 = f32[32,256,768]{1,0,2:T(8,128)} copy(f32[32,256,768]{2,1,0:T(8,128)} %param.4) | data formatting | bytes 50331648 | tf_op args[0]
  50.8 48.8 %all-reduce.3.cloned.1.call-done = (f32[32,768]{1,0:T(8,128)}, f32[32,768]{1,0:T(8,128)}) async-done(((f32[32,768]{1,0:T(8,128)}, f32[32,768]{1,0:T(8,128)}), (f32[32,768]{1,0:T(8,128)}, f32[32,768]{1,0:T(8,128)})) %all-reduce.3.cloned.1.call-update) | async-done | bytes 196624 | tf_op jit(solution)/shard_map/pmax | solution.py:8
  99.6 1.1 copy.20
  100.7 14.1 %divide_convert_fusion.1 = bf16[32,256,768]{1,0,2:T(8,128)(2,1)} fusion(f32[32,256,768]{1,0,2:T(8,128)} %copy.21, f32[32,768]{0,1:T(8,128)S(1)} %copy.20), kind=kLoop, calls=%fused_computation.2 | loop fusion | flops 12582912 | bytes 37847040 | tf_op jit(solution)/shard_map/convert_element_type | solution.py:12
  114.8 5.4 all-to-all-start
  120.2 0.0 copy-start.1
  120.2 25.1 %copy.25 = f32[32,256,768]{1,0,2:T(8,128)} copy(f32[32,256,768]{2,1,0:T(8,128)} %param.5) | data formatting | bytes 50331648 | tf_op args[1]
  145.3 0.0 copy-done.1
  145.3 0.2 copy.24
  145.5 0.0 copy-start.2
  145.5 0.0 copy-start.3
  145.5 14.1 %divide_convert_fusion = bf16[32,256,768]{1,0,2:T(8,128)(2,1)} fusion(f32[32,256,768]{1,0,2:T(8,128)} %copy.25, f32[32,768]{0,1:T(8,128)S(1)} %copy.24), kind=kLoop, calls=%fused_computation | loop fusion | flops 12582912 | bytes 37847040 | tf_op jit(solution)/shard_map/convert_element_type | solution.py:13
  159.6 231.8 %all-to-all-done = bf16[32,256,768]{1,0,2:T(8,128)(2,1)} async-done(((bf16[32,256,768]{1,0,2:T(8,128)(2,1)}), bf16[32,256,768]{1,0,2:T(8,128)(2,1)}, u32[]{:S(2)}, u32[]{:S(2)}) %all-to-all-start) | async-done | bytes 12582944 | tf_op jit(solution)/shard_map/all_to_all | solution.py:16
  391.4 5.3 all-to-all-start.1
  396.7 0.0 copy-done.2
  396.7 0.0 copy-done.3
  396.8 291.6 %all_gather.6 = bf16[2048,32]{0,1:T(8,128)(2,1)S(1)} all-gather(bf16[256,32]{0,1:T(8,128)(2,1)S(1)} %multiply_convert_fusion), channel_id=1, replica_groups=mesh['expert'=4,'shard'=8] {'shard'}, dimensions={0}, use_global_device_ids=true | all-gather | bytes 147456 | tf_op jit(solution)/shard_map/all_gather | solution.py:26
  688.4 7.1 all_gather.7
  695.5 1.0 copy.28
  696.5 1.4 constant_dynamic-slice_fusion
  698.0 14.1 %copy.23 = bf16[32,8,256,96]{2,1,3,0:T(8,128)(2,1)} copy(bf16[32,8,256,96]{2,0,3,1:T(8,128)(2,1)} %bitcast.2) | data formatting | bytes 25165824 | tf_op jit(solution)/shard_map/all_to_all | solution.py:16
  712.0 19.5 %all_to_all.29 = bf16[32,2048,96]{1,2,0:T(8,128)(2,1)} reshape(bf16[32,8,256,96]{2,1,3,0:T(8,128)(2,1)} %copy.23) | data formatting | bytes 25165824 | tf_op jit(solution)/shard_map/all_to_all | solution.py:16
  731.5 0.0 all-to-all-done.1
  731.5 14.1 %copy.27 = bf16[32,8,256,96]{2,1,3,0:T(8,128)(2,1)} copy(bf16[32,8,256,96]{2,0,3,1:T(8,128)(2,1)} %bitcast.5) | data formatting | bytes 25165824 | tf_op jit(solution)/shard_map/all_to_all | solution.py:17
  745.6 19.5 %all_to_all.33 = bf16[32,2048,96]{1,2,0:T(8,128)(2,1)} reshape(bf16[32,8,256,96]{2,1,3,0:T(8,128)(2,1)} %copy.27) | data formatting | bytes 25165824 | tf_op jit(solution)/shard_map/all_to_all | solution.py:17
  (1 shorter events, 0.0 us)
Async XLA Ops:
  7.2 92.4 %all-reduce.3.cloned.1.call-start = ((), (), s32[]{:S(2)}) async-start(), calls=%async_computation.2 | async-start | bytes 393216 | tf_op jit(solution)/shard_map/pmax | solution.py:8
  7.2 15.5 %copy-start = (f32[32,256,768]{2,1,0:T(8,128)S(1)}, f32[32,256,768]{2,1,0:T(8,128)}, u32[]{:S(2)}) copy-start(f32[32,256,768]{2,1,0:T(8,128)} %param.4) | copy-start | bytes 75497472
  114.8 276.6 %all-to-all-start = ((bf16[32,256,768]{1,0,2:T(8,128)(2,1)}), bf16[32,256,768]{1,0,2:T(8,128)(2,1)}, u32[]{:S(2)}, u32[]{:S(2)}) async-start(bf16[32,256,768]{1,0,2:T(8,128)(2,1)} %divide_convert_fusion.1), calls=%async_computation | async-start | bytes 25165824 | tf_op jit(solution)/shard_map/all_to_all | solution.py:16
  120.2 25.1 %copy-start.1 = (f32[32,768]{1,0:T(8,128)S(1)}, f32[32,768]{1,0:T(8,128)}, u32[]{:S(2)}) copy-start(f32[32,768]{1,0:T(8,128)} %get-tuple-element.11) | copy-start | bytes 294916
  145.5 251.3 %copy-start.2 = (f32[256,32]{0,1:T(8,128)S(1)}, f32[256,32]{0,1:T(8,128)}, u32[]{:S(2)}) copy-start(f32[256,32]{0,1:T(8,128)} %param.6) | copy-start | bytes 98308
  145.5 251.3 %copy-start.3 = (f32[256]{0:T(256)S(1)}, f32[256]{0:T(256)}, u32[]{:S(2)}) copy-start(f32[256]{0:T(256)} %param.7) | copy-start | bytes 3076
  391.4 340.1 %all-to-all-start.1 = ((bf16[32,256,768]{1,0,2:T(8,128)(2,1)}), bf16[32,256,768]{1,0,2:T(8,128)(2,1)}, u32[]{:S(2)}, u32[]{:S(2)}) async-start(bf16[32,256,768]{1,0,2:T(8,128)(2,1)} %divide_convert_fusion), calls=%async_computation.1 | async-start | bytes 25165824 | tf_op jit(solution)/shard_map/all_to_all | solution.py:17
Sparse Core Ops, SparseCore 0:
  25.9 73.6 all-reduce.2
where the time goes:
time: 774 us; the launch traced here: 772 us
  blocking collectives  299 us (39%)
  waiting for transfers between devices  281 us (36%)
  local copies, waits for them, and re-layouts  126 us (16%)
  other arithmetic  41.5 us (5%)
  between operations  14.1 us (2%)
  starting transfers between devices  10.8 us (1%)
    all_gather x1, blocking collectives, body(): row_router = lax.all_gather(part_router, 'shard', axis=0, tiled=True)  292 us
    all_to_all x1, waiting for transfers between devices, body(): lax.all_to_all(narrow_gate, 'shard', split_axis=2, concat_axis=1, tiled=T...  232 us
    unnamed x11, local copies, waits for them, and re-layouts  56.4 us
    pmax x1, waiting for transfers between devices, body(): lax.pmax((jnp.max(jnp.abs(w_gate), axis=1), jnp.max(jnp.abs(w_up), axis=1...  48.8 us
    all_to_all x2, local copies, waits for them, and re-layouts, body(): lax.all_to_all(narrow_up, 'shard', split_axis=2, concat_axis=1, tiled=True)  33.6 us
    all_to_all x2, local copies, waits for them, and re-layouts, body(): lax.all_to_all(narrow_gate, 'shard', split_axis=2, concat_axis=1, tiled=T...  33.5 us
  transfers between devices with their start and end apart: 3, of which 2 were waited for; matrix products, arithmetic and copies ran while one was open for 10% of the time, Pallas kernels for 0%

commit v1 on v0

--- a/solution.py
+++ b/solution.py
@@ -13,7 +13,12 @@
         (w_up / jnp.expand_dims(scale_up, 1)).astype(jnp.bfloat16),
     )
     serve_gate, serve_up = (
-        lax.all_to_all(narrow_gate, "shard", split_axis=2, concat_axis=1, tiled=True),
+        jnp.concatenate(
+            lax.all_to_all(
+                jnp.stack(jnp.split(narrow_gate, lax.axis_size("shard"), axis=2)), "shard", 0, 0
+            ),
+            axis=1,
+        ),
         lax.all_to_all(narrow_up, "shard", split_axis=2, concat_axis=1, tiled=True),
     )
     scale_gate = lax.dynamic_slice_in_dim(

time: 774 us -> 756 us (0.977)
  local copies, waits for them, and re-layouts: 126 us -> 112 us
    all_to_all x2 -> x0, local copies, waits for them, and re-layouts: 33.5 us -> none  [body(): lax.all_to_all(narrow_gate, 'shard', split_axis=2, concat_axis=1, tiled=T...]
    reshape x0 -> x1, local copies, waits for them, and re-layouts: none -> 10.9 us  [body(): jnp.concatenate(lax.all_to_all(jnp.stack(jnp.split(narrow_gate, lax.axis_...]
    unnamed x11 -> x18, local copies, waits for them, and re-layouts: 56.4 us -> 65 us
where the time goes in v1:
time: 756 us; the launch traced here: 755 us
  blocking collectives  299 us (40%)
  waiting for transfers between devices  281 us (37%)
  local copies, waits for them, and re-layouts  112 us (15%)
  other arithmetic  37.6 us (5%)
  between operations  14.1 us (2%)
  starting transfers between devices  10.8 us (1%)
    all_gather x1, blocking collectives, body(): row_router = lax.all_gather(part_router, 'shard', axis=0, tiled=True)  292 us
    all_to_all x1, waiting for transfers between devices, body(): lax.all_to_all(jnp.stack(jnp.split(narrow_gate, lax.axis_size('shard'), a...  232 us
    unnamed x18, local copies, waits for them, and re-layouts  65 us
    pmax x1, waiting for transfers between devices, body(): lax.pmax((jnp.max(jnp.abs(w_gate), axis=1), jnp.max(jnp.abs(w_up), axis=1...  49.2 us
    all_to_all x2, local copies, waits for them, and re-layouts, body(): lax.all_to_all(narrow_up, 'shard', split_axis=2, concat_axis=1, tiled=True)  33.6 us
  transfers between devices with their start and end apart: 3, of which 2 were waited for; matrix products, arithmetic and copies ran while one was open for 10% of the time, Pallas kernels for 0%

profile of v1, /device:TPU:0, one launch (start us, length us, event | category | flops | bytes accessed | tf_op | source)
XLA Modules:
  0.0 754.6 jit_solution(8349729934143389127)
XLA Ops:
  7.2 0.0 all-reduce.3.cloned.1.call-start
  7.2 0.0 copy-start
  7.2 10.2 %abs_reduce_fusion = f32[32,768]{1,0:T(8,128)} fusion(f32[32,256,768]{2,1,0:T(8,128)} %param.5), kind=kLoop, calls=%fused_computation.1 | loop fusion | flops 12558336 | bytes 25264128 | tf_op jit(solution)/shard_map/reduce_max | solution.py:9
  17.4 5.3 copy-done
  22.7 3.0 abs_reduce_fusion.1
  25.7 0.0 all-reduce.3.cloned.1.call-update
  25.7 24.7 %copy.25 = f32[32,256,768]{1,2,0:T(8,128)} copy(f32[32,256,768]{2,1,0:T(8,128)} %param.4) | data formatting | bytes 50331648 | tf_op args[0]
  50.4 49.2 %all-reduce.3.cloned.1.call-done = (f32[32,768]{1,0:T(8,128)}, f32[32,768]{1,0:T(8,128)}) async-done(((f32[32,768]{1,0:T(8,128)}, f32[32,768]{1,0:T(8,128)}), (f32[32,768]{1,0:T(8,128)}, f32[32,768]{1,0:T(8,128)})) %all-reduce.3.cloned.1.call-update) | async-done | bytes 196624 | tf_op jit(solution)/shard_map/pmax | solution.py:8
  99.6 10.3 %divide_convert_fusion.1 = bf16[32,256,768]{1,2,0:T(8,128)(2,1)S(1)} fusion(f32[32,256,768]{1,2,0:T(8,128)} %copy.25, f32[32,768]{1,0:T(8,128)} %get-tuple-element.15), kind=kLoop, calls=%fused_computation.2 | loop fusion | flops 12582912 | bytes 37847040 | tf_op jit(solution)/shard_map/convert_element_type | solution.py:12
  109.9 1.3 fusion.7
  111.2 1.3 fusion.6
  112.5 1.3 fusion.5
  113.8 1.3 fusion.4
  115.0 1.3 fusion.3
  116.3 1.3 fusion.2
  117.6 1.3 fusion.1
  118.9 1.3 fusion
  120.1 5.4 all-to-all-start
  125.6 0.0 copy-start.1
  125.6 25.1 %copy.28 = f32[32,256,768]{1,0,2:T(8,128)} copy(f32[32,256,768]{2,1,0:T(8,128)} %param.5) | data formatting | bytes 50331648 | tf_op args[1]
  150.6 0.2 copy.27
  150.8 14.1 %divide_convert_fusion = bf16[32,256,768]{1,0,2:T(8,128)(2,1)} fusion(f32[32,256,768]{1,0,2:T(8,128)} %copy.28, f32[32,768]{0,1:T(8,128)S(1)} %copy.27), kind=kLoop, calls=%fused_computation | loop fusion | flops 12582912 | bytes 37847040 | tf_op jit(solution)/shard_map/convert_element_type | solution.py:13
  164.9 231.8 %all-to-all-done = bf16[8,32,256,96]{2,3,1,0:T(8,128)(2,1)} async-done(((bf16[8,32,256,96]{2,3,1,0:T(8,128)(2,1)}), bf16[8,32,256,96]{2,3,1,0:T(8,128)(2,1)}, u32[]{:S(2)}, u32[]{:S(2)}) %all-to-all-start) | async-done | bytes 12582944 | tf_op jit(solution)/shard_map/all_to_all | solution.py:17
  396.7 5.3 all-to-all-start.1
  402.1 291.6 %all_gather.6 = bf16[2048,32]{0,1:T(8,128)(2,1)S(1)} all-gather(bf16[256,32]{0,1:T(8,128)(2,1)S(1)} %multiply_convert_fusion), channel_id=1, replica_groups=mesh['expert'=4,'shard'=8] {'shard'}, dimensions={0}, use_global_device_ids=true | all-gather | bytes 147456 | tf_op jit(solution)/shard_map/all_gather | solution.py:31
  693.7 7.1 all_gather.7
  700.9 1.0 copy.31
  701.9 1.4 constant_dynamic-slice_fusion
  703.3 10.9 %copy.33 = bf16[8,32,12,8,256]{4,3,0,2,1:T(8,128)(2,1)} copy(bf16[8,32,12,8,256]{4,3,2,1,0:T(8,128)(2,1)} %bitcast.12) | data formatting | bytes 25165824 | tf_op jit(solution)/shard_map/reshape | solution.py:16
  714.2 0.0 all-to-all-done.1
  714.2 14.1 %copy.30 = bf16[32,8,256,96]{2,1,3,0:T(8,128)(2,1)} copy(bf16[32,8,256,96]{2,0,3,1:T(8,128)(2,1)} %bitcast.11) | data formatting | bytes 25165824 | tf_op jit(solution)/shard_map/all_to_all | solution.py:22
  728.3 19.5 %all_to_all.20 = bf16[32,2048,96]{1,2,0:T(8,128)(2,1)} reshape(bf16[32,8,256,96]{2,1,3,0:T(8,128)(2,1)} %copy.30) | data formatting | bytes 25165824 | tf_op jit(solution)/shard_map/all_to_all | solution.py:22
  (6 shorter events, 0.0 us)
Async XLA Ops:
  7.2 92.5 %all-reduce.3.cloned.1.call-start = ((), (), s32[]{:S(2)}) async-start(), calls=%async_computation.2 | async-start | bytes 393216 | tf_op jit(solution)/shard_map/pmax | solution.py:8
  7.2 15.5 %copy-start = (f32[32,256,768]{2,1,0:T(8,128)S(1)}, f32[32,256,768]{2,1,0:T(8,128)}, u32[]{:S(2)}) copy-start(f32[32,256,768]{2,1,0:T(8,128)} %param.4) | copy-start | bytes 75497472
  120.1 276.6 %all-to-all-start = ((bf16[8,32,256,96]{2,3,1,0:T(8,128)(2,1)}), bf16[8,32,256,96]{2,3,1,0:T(8,128)(2,1)}, u32[]{:S(2)}, u32[]{:S(2)}) async-start(bf16[8,32,256,96]{2,3,1,0:T(8,128)(2,1)} %fusion), calls=%async_computation | async-start | bytes 25165824 | tf_op jit(solution)/shard_map/all_to_all | solution.py:17
  125.6 25.1 %copy-start.1 = (f32[32,768]{1,0:T(8,128)S(1)}, f32[32,768]{1,0:T(8,128)}, u32[]{:S(2)}) copy-start(f32[32,768]{1,0:T(8,128)} %get-tuple-element.16) | copy-start | bytes 294916
  164.9 237.2 %copy-start.2 = (f32[256,32]{0,1:T(8,128)S(1)}, f32[256,32]{0,1:T(8,128)}, u32[]{:S(2)}) copy-start(f32[256,32]{0,1:T(8,128)} %param.6) | copy-start | bytes 98308
  164.9 237.2 %copy-start.3 = (f32[256]{0:T(256)S(1)}, f32[256]{0:T(256)}, u32[]{:S(2)}) copy-start(f32[256]{0:T(256)} %param.7) | copy-start | bytes 3076
  396.7 317.4 %all-to-all-start.1 = ((bf16[32,256,768]{1,0,2:T(8,128)(2,1)}), bf16[32,256,768]{1,0,2:T(8,128)(2,1)}, u32[]{:S(2)}, u32[]{:S(2)}) async-start(bf16[32,256,768]{1,0,2:T(8,128)(2,1)} %divide_convert_fusion), calls=%async_computation.1 | async-start | bytes 25165824 | tf_op jit(solution)/shard_map/all_to_all | solution.py:22
Sparse Core Ops, SparseCore 0:
  25.9 73.7 all-reduce.2
